TPU v7x, 256 devices: a whole 4x4x8 slice. The times are simulated.
256 devices in a mesh: row: 16 (over z, x_lo), col: 8 (over y, x_hi), depth: 2 (over core).
Axes of the slice: x: 4 (x_hi: 2, x_lo: 2; x = x_hi * 2 + x_lo), y: 4, z: 8, core: 2. Of those that a mesh axis runs over, the one named last changes fastest.
Arguments:
- matrix: float32 [2, 16, 512, 4, 8, 512], P(None, 'row', None, None, 'col'), may hold values from 0 to 5
Outputs:
- factored: float32 [2, 16, 512, 4, 8, 512], P(None, 'row', 'depth', None, 'col')
All inputs are finite; a program needn't handle non-finite values.
Results may differ from a plain program's by a relative error of at most 0.00021.
Values sent between devices are 32-bit elements; how exact they have to be, the bound alone decides.
A program may use at most 128 MiB of HBM per device.

v0:
```python
import jax
import jax.numpy as jnp
from jax import lax
from jax.sharding import Mesh
from jax.sharding import PartitionSpec as P

STEPS = 2
ROW = ("row_0", "row_1")


def split_up(x, dim, size):
    before, after = (x.shape[:dim], x.shape[dim + 1 :])
    return jnp.moveaxis(x.reshape(*before, size, -1, *after), dim, 0)


def summed_on_arrival(x, axis, dim):
    blocks = split_up(x, dim, lax.axis_size(axis))
    arrived = lax.all_to_all(blocks, axis, split_axis=0, concat_axis=0, tiled=True)
    return arrived.sum(axis=0)


def spread(x, axes, root):
    x = jnp.where(lax.axis_index(axes) == root, x, jnp.zeros_like(x))
    for axis in axes:
        x = lax.psum(x, axis)
    return x


def from_everyone(x, axis):
    size = lax.axis_size(axis)
    return lax.all_to_all(jnp.broadcast_to(x[None], (size, *x.shape)), axis, 0, 0, tiled=True)


def laid_out(blocks, dim):
    shape = list(blocks.shape[1:])
    shape[dim] *= blocks.shape[0]
    return jnp.moveaxis(blocks, 0, dim).reshape(shape)


def gathered_copies(x, axis, dim):
    blocks = from_everyone(x, axis)
    return laid_out(blocks, dim)


def broadcast(x, axis, root):
    return lax.dynamic_index_in_dim(lax.all_gather(x, axis), root, 0, keepdims=False)


def body(matrix):
    tiles_rows = matrix.shape[0]
    tile = matrix.shape[2]
    tiles_cols = matrix.shape[3]
    grid_rows = lax.axis_size(ROW)
    grid_cols = lax.axis_size("col")
    layers_count = lax.axis_size("depth")
    half_width = tile // layers_count
    depth_index = lax.axis_index("depth")
    row_index = lax.axis_index(ROW)
    col_index = lax.axis_index("col")
    local = matrix.reshape(tiles_rows, tile, tiles_cols, tile)
    keeper = (depth_index == 0).astype(jnp.float32)
    columns = [local[:, :, j, :] * keeper for j in range(tiles_cols)]
    global_rows = jnp.arange(tiles_rows, dtype=jnp.int32) * grid_rows + row_index
    global_cols = jnp.arange(tiles_cols, dtype=jnp.int32) * grid_cols + col_index
    identity = jnp.eye(tile, dtype=jnp.float32)
    stored = []
    for section in range(STEPS):
        owner_col = section % grid_cols
        slot_col = section // grid_cols
        reduced = summed_on_arrival(columns[slot_col], "depth", 1)
        shared = broadcast(reduced, "col", owner_col)
        owner_row = section % grid_rows
        slot_row = section // grid_rows
        halves = spread(shared[slot_row], ROW, owner_row)
        diag = gathered_copies(halves, "depth", 0)
        diag_factor = jnp.linalg.cholesky(diag)
        inverse_factor = jax.scipy.linalg.solve_triangular(diag_factor, identity, lower=True)
        solved = jnp.einsum(
            "ipb,cb->ipc",
            shared,
            inverse_factor,
            precision=lax.Precision.HIGHEST,
            preferred_element_type=jnp.float32,
        )
        own_rows = lax.dynamic_slice_in_dim(diag_factor, depth_index * half_width, half_width, 0)
        below = (global_rows > section)[:, None, None]
        at_diag = (global_rows == section)[:, None, None]
        panel = jnp.where(below, solved, jnp.where(at_diag, own_rows[None], 0.0))
        rows_half = lax.all_to_all(panel, "depth", split_axis=2, concat_axis=1, tiled=True)
        stored.append(panel)
        rows_half = rows_half * (global_rows > section).astype(jnp.float32)[:, None, None]
        tiles_out = []
        for crossing_j in range(tiles_cols):
            target = global_cols[crossing_j]
            owner = target % grid_rows
            slot = target // grid_rows
            piece = lax.dynamic_index_in_dim(rows_half, slot, 0, keepdims=False)
            tiles_out.append(spread(piece, ROW, owner))
        for j in range(tiles_cols):
            columns[j] = columns[j] - jnp.einsum(
                "ipe,qe->ipq",
                rows_half,
                tiles_out[j],
                precision=lax.Precision.HIGHEST,
                preferred_element_type=jnp.float32,
            )
    whole = jnp.stack(columns, axis=2)
    summed = summed_on_arrival(whole, "depth", 1)
    upper = (global_rows < STEPS)[:, None, None, None] & (global_cols >= STEPS)[None, None, :, None]
    summed = jnp.where(upper, 0.0, summed)
    for section in range(STEPS):
        owner_col = section % grid_cols
        slot_col = section // grid_cols
        hit = col_index == owner_col
        summed = summed.at[:, :, slot_col, :].set(
            jnp.where(hit, stored[section], summed[:, :, slot_col, :])
        )
    return summed.reshape(tiles_rows, 1, half_width, tiles_cols, 1, tile)


def solution(mesh):
    split = Mesh(
        mesh.devices.reshape(8, 2, mesh.shape["col"], mesh.shape["depth"]),
        ("row_0", "row_1", "col", "depth"),
    )
    placed = (P(None, ROW, None, None, "col", None),)
    return jax.shard_map(
        body,
        mesh=split,
        in_specs=placed,
        out_specs=P(None, ROW, "depth", None, "col", None),
        check_vma=False,
    )
```

profile of v0, /device:TPU:1, one launch (start us, length us, event | category | flops | bytes accessed | tf_op | source)
XLA Modules:
  0.0 1221.9 jit_solution(510988850766627012)
XLA Ops:
  6.5 6.1 copy.39
  12.6 3.2 copy-done
  17.6 8.1 all-to-all-start
  25.6 2.6 all-to-all-done
  28.3 2.9 reduce_sum.29
  31.2 111.9 %all-gather.5.cloned.1.call-done = f32[16,256,512]{2,1,0:T(8,128)} async-done(((f32[2,256,512]{2,1,0:T(8,128)}), f32[16,256,512]{2,1,0:T(8,128)}) %all-gather.5.cloned.1.call-update) | async-done | bytes 8388624 | tf_op jit(solution)/shard_map/all_gather | solution.py:46
  143.1 1.9 fusion.40
  145.1 68.1 %all-reduce.12.cloned.1.call-done = f32[256,512]{1,0:T(8,128)} async-done(((f32[256,512]{1,0:T(8,128)}), f32[256,512]{1,0:T(8,128)}) %all-reduce.12.cloned.1.call-update) | async-done | bytes 524304 | tf_op jit(solution)/shard_map/psum | solution.py:25
  225.6 33.4 %all-reduce.14.cloned.1.call-done = f32[256,512]{1,0:T(8,128)} async-done(((f32[256,512]{1,0:T(8,128)}), f32[256,512]{1,0:T(8,128)}) %all-reduce.14.cloned.1.call-update) | async-done | bytes 524304 | tf_op jit(solution)/shard_map/psum | solution.py:25
  260.4 5.0 all_to_all.61
  269.3 11.7 cholesky.286
  281.0 9.8 custom-call.27
  293.5 11.7 cholesky.305
  305.3 10.0 custom-call.28
  316.8 11.7 cholesky.326
  329.3 9.8 custom-call.29
  340.5 11.7 cholesky.343
  356.3 3.2 fusion.27
  359.6 11.0 while.6
  360.2 2.2 bitcast_dynamic-update-slice_fusion.6
  362.9 2.2 bitcast_dynamic-update-slice_fusion.6
  365.7 2.2 bitcast_dynamic-update-slice_fusion.6
  368.5 2.1 bitcast_dynamic-update-slice_fusion.6
  371.3 40.1 %custom-call.30 = f32[4,128,128]{1,2,0:T(8,128)S(1)} custom-call(f32[4,128,128]{2,1,0:T(8,128)} %copy-done.18), custom_call_target="InvertDiagBlocksLowerTriangular" | custom-call | tf_op jit(solution)/shard_map/jit(_solve_triangular)/triangular_solve | solution.py:77
  417.4 3.1 convolution_select_fusion.1
  421.8 6.6 all_to_all.62
  428.5 2.3 copy.18
  433.5 69.9 %all-reduce.16.cloned.1.call-done = f32[512,256]{1,0:T(8,128)} async-done(((f32[512,256]{1,0:T(8,128)}), f32[512,256]{1,0:T(8,128)}) %all-reduce.16.cloned.1.call-update) | async-done | bytes 524304 | tf_op jit(solution)/shard_map/psum | solution.py:25
  503.4 45.6 %all-reduce.18.cloned.1.call-done = f32[512,256]{1,0:T(8,128)} async-done(((f32[512,256]{1,0:T(8,128)}), f32[512,256]{1,0:T(8,128)}) %all-reduce.18.cloned.1.call-update) | async-done | bytes 524304 | tf_op jit(solution)/shard_map/psum | solution.py:25
  549.0 3.0 bitcast_subtract_fusion
  553.3 5.9 all_to_all.63
  560.6 111.7 %all-gather.7.cloned.1.call-done = f32[16,256,512]{2,1,0:T(8,128)} async-done(((f32[2,256,512]{2,1,0:T(8,128)}), f32[16,256,512]{2,1,0:T(8,128)}) %all-gather.7.cloned.1.call-update) | async-done | bytes 8388624 | tf_op jit(solution)/shard_map/all_gather | solution.py:46
  672.2 1.9 fusion.39
  674.2 68.1 %all-reduce.20.cloned.1.call-done = f32[256,512]{1,0:T(8,128)} async-done(((f32[256,512]{1,0:T(8,128)}), f32[256,512]{1,0:T(8,128)}) %all-reduce.20.cloned.1.call-update) | async-done | bytes 524304 | tf_op jit(solution)/shard_map/psum | solution.py:25
  742.4 45.7 %all-reduce.22.cloned.1.call-done = f32[256,512]{1,0:T(8,128)} async-done(((f32[256,512]{1,0:T(8,128)}), f32[256,512]{1,0:T(8,128)}) %all-reduce.22.cloned.1.call-update) | async-done | bytes 524304 | tf_op jit(solution)/shard_map/psum | solution.py:25
  789.4 5.0 all_to_all.64
  796.2 11.7 cholesky.358
  808.1 9.8 custom-call.31
  820.4 11.7 cholesky.377
  833.4 10.0 custom-call.32
  845.0 11.7 cholesky.398
  857.5 9.8 custom-call.33
  868.7 11.7 cholesky.415
  883.7 2.0 fusion.25
  885.7 11.3 while.7
  886.3 2.2 bitcast_dynamic-update-slice_fusion.7
  889.2 2.2 bitcast_dynamic-update-slice_fusion.7
  892.0 2.2 bitcast_dynamic-update-slice_fusion.7
  894.9 2.1 bitcast_dynamic-update-slice_fusion.7
  897.0 39.3 %custom-call.34 = f32[4,128,128]{1,2,0:T(8,128)S(1)} custom-call(f32[4,128,128]{2,1,0:T(8,128)S(1)} %get-tuple-element.46), custom_call_target="InvertDiagBlocksLowerTriangular" | custom-call | tf_op jit(solution)/shard_map/jit(_solve_triangular)/triangular_solve | solution.py:77
  942.2 3.1 convolution_select_fusion
  946.7 5.7 all_to_all.65
  956.8 100.1 %all-reduce.24.cloned.1.call-done = (f32[512,256]{1,0:T(8,128)}, f32[512,256]{1,0:T(8,128)}, f32[512,256]{1,0:T(8,128)}, f32[512,256]{1,0:T(8,128)}, f32[512,256...) async-done(((f32[512,256]{1,0:T(8,128)}, f32[512,256]{1,0:T(8,128)}, f32[512,256]{1,0:T(8,128)}, f32[512,256]{1,0:T(8,128)}, f32[512,256]{1,0:T(8,128)}, ...) | async-done | bytes 3670032 | tf_op jit(solution)/shard_map/psum | solution.py:25
  1057.1 110.7 %all-reduce.26.cloned.1.call-done = (f32[512,256]{1,0:T(8,128)}, f32[512,256]{1,0:T(8,128)}, f32[512,256]{1,0:T(8,128)}, f32[512,256]{1,0:T(8,128)}, f32[512,256...) async-done(((f32[512,256]{1,0:T(8,128)}, f32[512,256]{1,0:T(8,128)}, f32[512,256]{1,0:T(8,128)}, f32[512,256]{1,0:T(8,128)}, f32[512,256]{1,0:T(8,128)}, ...) | async-done | bytes 3670032 | tf_op jit(solution)/shard_map/psum | solution.py:25
  1167.8 3.7 convolution_subtract_fusion
  1171.5 1.9 fusion.54
  1173.4 1.9 fusion.51
  1177.2 2.1 fusion.8
  1179.4 2.1 fusion.5
  1181.6 2.4 fusion.2
  1185.0 12.2 %all_to_all.66 = f32[2,2,256,4,512]{4,2,1,3,0:T(8,128)} all-to-all(f32[2,2,256,4,512]{4,2,1,3,0:T(8,128)S(1)} %copy_bitcast_fusion), channel_id=1, replica_groups=mesh['row_0'=8,'row_1'=2,'col'=8,'depth'=2] {'depth'}, dimensions={0} | all-to-all | bytes 16777216 | tf_op jit(solution)/shard_map/all_to_all | solution.py:18
  1197.2 6.9 reduce_sum.31
  1204.0 2.9 bitcast_select_fusion
  1208.5 6.3 copy.31
  (168 shorter events, 62.8 us)
Async XLA Ops:
  12.6 3.2 copy-start
  17.6 10.7 all-to-all-start
  25.6 117.5 %all-gather.5.cloned.1.call-start = ((), (), s32[]{:S(2)}) async-start(), calls=%async_computation.13 | async-start | bytes 9437184 | tf_op jit(solution)/shard_map/all_gather | solution.py:46
  31.2 182.1 %all-reduce.12.cloned.1.call-start = ((), (), s32[]{:S(2)}) async-start(), calls=%async_computation.7 | async-start | bytes 1048576 | tf_op jit(solution)/shard_map/psum | solution.py:25
  145.0 114.0 %all-reduce.14.cloned.1.call-start = ((), (), s32[]{:S(2)}) async-start(), calls=%async_computation.8 | async-start | bytes 1048576 | tf_op jit(solution)/shard_map/psum | solution.py:25
  213.2 290.1 %all-reduce.16.cloned.1.call-start = ((), (), s32[]{:S(2)}) async-start(), calls=%async_computation.9 | async-start | bytes 1048576 | tf_op jit(solution)/shard_map/psum | solution.py:25
  268.3 1.0 copy-start.9
  352.3 4.0 copy-start.7
  356.3 55.2 %copy-start.5 = (f32[512,512]{1,0:T(8,128)S(1)}, f32[512,512]{1,0:T(8,128)}, u32[]{:S(2)}) copy-start(f32[512,512]{1,0:T(8,128)} %fusion.28) | copy-start | bytes 3145732
  370.6 0.7 copy-start.18
  413.1 4.2 copy-start.11
  420.5 7.9 copy-start.3
  433.5 115.6 %all-reduce.18.cloned.1.call-start = ((), (), s32[]{:S(2)}) async-start(), calls=%async_computation.10 | async-start | bytes 1048576 | tf_op jit(solution)/shard_map/psum | solution.py:25
  503.4 168.8 %all-gather.7.cloned.1.call-start = ((), (), s32[]{:S(2)}) async-start(), calls=%async_computation.14 | async-start | bytes 9437184 | tf_op jit(solution)/shard_map/all_gather | solution.py:46
  552.0 1.3 copy-start.2
  560.5 181.8 %all-reduce.20.cloned.1.call-start = ((), (), s32[]{:S(2)}) async-start(), calls=%async_computation.11 | async-start | bytes 1048576 | tf_op jit(solution)/shard_map/psum | solution.py:25
  674.1 114.0 %all-reduce.22.cloned.1.call-start = ((), (), s32[]{:S(2)}) async-start(), calls=%async_computation.12 | async-start | bytes 1048576 | tf_op jit(solution)/shard_map/psum | solution.py:25
  742.3 314.6 %all-reduce.24.cloned.1.call-start = ((), (), s32[]{:S(2)}) async-start(), calls=%async_computation.15 | async-start | bytes 7340032 | tf_op jit(solution)/shard_map/psum | solution.py:25
  795.2 1.0 copy-start.8
  883.6 52.7 %copy-start.6 = (f32[512,512]{1,0:T(8,128)S(1)}, f32[512,512]{1,0:T(8,128)}, u32[]{:S(2)}) copy-start(f32[512,512]{1,0:T(8,128)} %fusion.28) | copy-start | bytes 3145732
  938.0 4.2 copy-start.10
  956.6 211.2 %all-reduce.26.cloned.1.call-start = ((), (), s32[]{:S(2)}) async-start(), calls=%async_computation.16 | async-start | bytes 7340032 | tf_op jit(solution)/shard_map/psum | solution.py:25
  1167.8 3.8 copy-start.17
  1167.8 9.4 slice-start
  1171.5 1.9 copy-start.16
  1171.5 5.7 slice-start.1
  1173.4 1.9 copy-start.15
  1175.3 1.9 copy-start.14
  1177.2 2.2 copy-start.13
  1179.4 2.2 copy-start.12
  1204.0 3.4 copy-start.1
  1204.0 3.7 copy-start.4
Sparse Core Ops, SparseCore 0:
  31.3 111.8 all-gather.4
  145.5 67.7 all-reduce.11
  215.8 43.1 all-reduce.13
  433.6 69.7 all-reduce.15
  505.8 43.1 all-reduce.17
  560.6 111.5 all-gather.6
  674.5 67.7 all-reduce.19
  744.9 43.1 all-reduce.21
  956.7 100.2 all-reduce.23
  1059.9 107.8 all-reduce.25
where the time goes:
time: 1230 us; the launch traced here: 1220 us
  waiting for transfers between devices  768 us (62%)
  other arithmetic  271 us (22%)
  local copies, waits for them, and re-layouts  56.1 us (5%)
  matrix products  47.6 us (4%)
  blocking collectives  40.5 us (3%)
  between operations  30.2 us (2%)
    psum x8, waiting for transfers between devices, spread(): x = lax.psum(x, axis)  542 us
    all_gather x2, waiting for transfers between devices, broadcast(): lax.all_gather(x, axis)  224 us
    another operation x29, other arithmetic, body(): diag_factor = jnp.linalg.cholesky(diag)  158 us
    another operation x5, other arithmetic, body(): jax.scipy.linalg.solve_triangular(diag_factor, identity, lower=True)  84.6 us
  transfers between devices with their start and end apart: 11, of which 11 were waited for; matrix products, arithmetic and copies ran while one was open for 0% of the time, Pallas kernels for 0%

commit v1 on v0

--- a/solution.py
+++ b/solution.py
@@ -22,7 +22,7 @@
 def spread(x, axes, root):
     x = jnp.where(lax.axis_index(axes) == root, x, jnp.zeros_like(x))
     for axis in axes:
-        x = lax.psum(x, axis)
+        x = jnp.sum(lax.all_gather(x, axis), axis=0)
     return x
 
 

time: 1230 us -> 1340 us (1.089)
  other arithmetic: 271 us -> 321 us
  waiting for transfers between devices: 768 us -> 812 us
  matrix products: 47.6 us -> 62.2 us
    all_gather x0 -> x20, waiting for transfers between devices: none -> 582 us  [spread(): x = jnp.sum(lax.all_gather(x, axis), axis=0)]
    psum x8 -> x0, waiting for transfers between devices: 542 us -> none  [spread(): x = lax.psum(x, axis)]
    reduce_sum x0 -> x20, other arithmetic: none -> 51.1 us  [spread(): x = jnp.sum(lax.all_gather(x, axis), axis=0)]
    dot_general x8, matrix products: 18.9 us -> 33.5 us  [body(): jnp.einsum('ipe,qe->ipq', rows_half, tiles_out[j], precision=lax.Precisio...]
  transfers between devices with their start and end apart: 11 -> 23, of which waited for: 11 -> 20; matrix products, arithmetic and copies ran while one was open for 0% -> 16% of each run, Pallas kernels for 0% -> 0%
where the time goes in v1:
time: 1340 us; the launch traced here: 1330 us
  waiting for transfers between devices  812 us (61%)
  other arithmetic  321 us (24%)
  matrix products  62.2 us (5%)
  local copies, waits for them, and re-layouts  57 us (4%)
  blocking collectives  40.5 us (3%)
  between operations  30.4 us (2%)
    all_gather x20, waiting for transfers between devices, spread(): x = jnp.sum(lax.all_gather(x, axis), axis=0)  582 us
    all_gather x2, waiting for transfers between devices, broadcast(): lax.all_gather(x, axis)  224 us
    another operation x29, other arithmetic, body(): diag_factor = jnp.linalg.cholesky(diag)  158 us
    another operation x5, other arithmetic, body(): jax.scipy.linalg.solve_triangular(diag_factor, identity, lower=True)  84.3 us
    reduce_sum x20, other arithmetic, spread(): x = jnp.sum(lax.all_gather(x, axis), axis=0)  51.1 us
    dot_general x8, matrix products, body(): jnp.einsum('ipe,qe->ipq', rows_half, tiles_out[j], precision=lax.Precisio...  33.5 us
  transfers between devices with their start and end apart: 23, of which 20 were waited for; matrix products, arithmetic and copies ran while one was open for 16% of the time, Pallas kernels for 0%

profile of v1, /device:TPU:1, one launch (start us, length us, event | category | flops | bytes accessed | tf_op | source)
XLA Modules:
  0.0 1332.4 jit_solution(16974150120250580060)
XLA Ops:
  6.5 6.1 copy.55
  12.6 3.2 copy-done
  17.6 8.1 all-to-all-start
  31.2 111.9 %all-gather.53.cloned.1.call-done = f32[16,256,512]{2,1,0:T(8,128)} async-done(((f32[2,256,512]{2,1,0:T(8,128)}), f32[16,256,512]{2,1,0:T(8,128)}) %all-gather.53.cloned.1.call-update) | async-done | bytes 8388624 | tf_op jit(solution)/shard_map/all_gather | solution.py:46
  145.1 53.3 %all-gather.55.cloned.1.call-done = f32[8,1,256,512]{3,2,1,0:T(8,128)} async-done(((f32[1,1,256,512]{3,2,1,0:T(8,128)}), f32[8,1,256,512]{3,2,1,0:T(8,128)}) %all-gather.55.cloned.1.call-update) | async-done | bytes 4194320 | tf_op jit(solution)/shard_map/all_gather | solution.py:25
  198.4 3.5 reduce_sum.210
  214.0 13.1 all-gather.57.cloned.1.call-done
  230.5 5.0 all_to_all.61
  239.5 11.7 cholesky.286
  251.2 9.8 custom-call.27
  263.7 11.7 cholesky.305
  275.4 10.0 custom-call.28
  287.0 11.7 cholesky.326
  299.5 9.8 custom-call.29
  310.7 11.7 cholesky.343
  326.5 3.3 fusion.27
  329.8 11.1 while.6
  341.6 40.1 %custom-call.30 = f32[4,128,128]{1,2,0:T(8,128)S(1)} custom-call(f32[4,128,128]{2,1,0:T(8,128)} %copy-done.18), custom_call_target="InvertDiagBlocksLowerTriangular" | custom-call | tf_op jit(solution)/shard_map/jit(_solve_triangular)/triangular_solve | solution.py:77
  392.1 6.6 all_to_all.62
  403.8 55.4 %all-gather.37.cloned.1.call-done = f32[8,512,256]{2,1,0:T(8,128)} async-done(((f32[1,512,256]{2,1,0:T(8,128)}), f32[8,512,256]{2,1,0:T(8,128)}) %all-gather.37.cloned.1.call-update) | async-done | bytes 4194320 | tf_op jit(solution)/shard_map/all_gather | solution.py:25
  459.1 3.3 reduce_sum.212
  462.6 25.1 %all-gather.59.cloned.1.call-done = f32[1024,256]{1,0:T(8,128)} async-done(((f32[512,256]{1,0:T(8,128)}), f32[1024,256]{1,0:T(8,128)}) %all-gather.59.cloned.1.call-update) | async-done | bytes 1048592 | tf_op jit(solution)/shard_map/all_gather | solution.py:25
  494.1 5.9 all_to_all.63
  501.3 111.7 %all-gather.61.cloned.1.call-done = f32[16,256,512]{2,1,0:T(8,128)} async-done(((f32[2,256,512]{2,1,0:T(8,128)}), f32[16,256,512]{2,1,0:T(8,128)}) %all-gather.61.cloned.1.call-update) | async-done | bytes 8388624 | tf_op jit(solution)/shard_map/all_gather | solution.py:46
  614.9 53.3 %all-gather.63.cloned.1.call-done = f32[8,1,256,512]{3,2,1,0:T(8,128)} async-done(((f32[1,1,256,512]{3,2,1,0:T(8,128)}), f32[8,1,256,512]{3,2,1,0:T(8,128)}) %all-gather.63.cloned.1.call-update) | async-done | bytes 4194320 | tf_op jit(solution)/shard_map/all_gather | solution.py:25
  668.3 3.5 reduce_sum.215
  673.9 23.0 %all-gather.65.cloned.1.call-done = f32[512,512]{1,0:T(8,128)} async-done(((f32[256,512]{1,0:T(8,128)}), f32[512,512]{1,0:T(8,128)}) %all-gather.65.cloned.1.call-update) | async-done | bytes 1048592 | tf_op jit(solution)/shard_map/all_gather | solution.py:25
  698.5 5.0 all_to_all.64
  705.3 11.7 cholesky.358
  717.2 9.8 custom-call.31
  729.5 11.7 cholesky.377
  741.3 10.0 custom-call.32
  752.9 11.7 cholesky.398
  764.6 9.8 custom-call.33
  775.9 11.7 cholesky.415
  794.8 11.4 while.7
  806.3 39.3 %custom-call.34 = f32[4,128,128]{1,2,0:T(8,128)S(1)} custom-call(f32[4,128,128]{2,1,0:T(8,128)S(1)} %get-tuple-element.46), custom_call_target="InvertDiagBlocksLowerTriangular" | custom-call | tf_op jit(solution)/shard_map/jit(_solve_triangular)/triangular_solve | solution.py:77
  857.0 5.7 all_to_all.65
  868.2 3.3 reduce_sum.219
  871.6 3.3 reduce_sum.223
  875.0 3.3 reduce_sum.227
  879.0 43.2 %all-gather.39.cloned.1.call-done = f32[8,512,256]{2,1,0:T(8,128)} async-done(((f32[1,512,256]{2,1,0:T(8,128)}), f32[8,512,256]{2,1,0:T(8,128)}) %all-gather.39.cloned.1.call-update) | async-done | bytes 4194320 | tf_op jit(solution)/shard_map/all_gather | solution.py:25
  922.2 3.3 reduce_sum.217
  925.6 51.8 %all-gather.43.cloned.1.call-done = f32[8,512,256]{2,1,0:T(8,128)} async-done(((f32[1,512,256]{2,1,0:T(8,128)}), f32[8,512,256]{2,1,0:T(8,128)}) %all-gather.43.cloned.1.call-update) | async-done | bytes 4194320 | tf_op jit(solution)/shard_map/all_gather | solution.py:25
  977.4 3.3 reduce_sum.221
  980.8 51.6 %all-gather.47.cloned.1.call-done = f32[8,512,256]{2,1,0:T(8,128)} async-done(((f32[1,512,256]{2,1,0:T(8,128)}), f32[8,512,256]{2,1,0:T(8,128)}) %all-gather.47.cloned.1.call-update) | async-done | bytes 4194320 | tf_op jit(solution)/shard_map/all_gather | solution.py:25
  1032.4 3.3 reduce_sum.225
  1036.0 23.0 %all-gather.69.cloned.1.call-done = f32[1024,256]{1,0:T(8,128)} async-done(((f32[512,256]{1,0:T(8,128)}), f32[1024,256]{1,0:T(8,128)}) %all-gather.69.cloned.1.call-update) | async-done | bytes 1048592 | tf_op jit(solution)/shard_map/all_gather | solution.py:25
  1061.2 26.9 %all-gather.73.cloned.1.call-done = f32[1024,256]{1,0:T(8,128)} async-done(((f32[512,256]{1,0:T(8,128)}), f32[1024,256]{1,0:T(8,128)}) %all-gather.73.cloned.1.call-update) | async-done | bytes 1048592 | tf_op jit(solution)/shard_map/all_gather | solution.py:25
  1090.2 26.9 %all-gather.77.cloned.1.call-done = f32[1024,256]{1,0:T(8,128)} async-done(((f32[512,256]{1,0:T(8,128)}), f32[1024,256]{1,0:T(8,128)}) %all-gather.77.cloned.1.call-update) | async-done | bytes 1048592 | tf_op jit(solution)/shard_map/all_gather | solution.py:25
  1119.2 4.3 fusion.52
  1129.9 44.6 %all-gather.51.cloned.1.call-done = f32[8,512,256]{2,1,0:T(8,128)} async-done(((f32[1,512,256]{2,1,0:T(8,128)}), f32[8,512,256]{2,1,0:T(8,128)}) %all-gather.51.cloned.1.call-update) | async-done | bytes 4194320 | tf_op jit(solution)/shard_map/all_gather | solution.py:25
  1174.5 3.3 reduce_sum.229
  1177.8 23.5 %all-gather.67.cloned.1.call-done = f32[1024,256]{1,0:T(8,128)} async-done(((f32[512,256]{1,0:T(8,128)}), f32[1024,256]{1,0:T(8,128)}) %all-gather.67.cloned.1.call-update) | async-done | bytes 1048592 | tf_op jit(solution)/shard_map/all_gather | solution.py:25
  1203.4 26.9 %all-gather.71.cloned.1.call-done = f32[1024,256]{1,0:T(8,128)} async-done(((f32[512,256]{1,0:T(8,128)}), f32[1024,256]{1,0:T(8,128)}) %all-gather.71.cloned.1.call-update) | async-done | bytes 1048592 | tf_op jit(solution)/shard_map/all_gather | solution.py:25
  1231.7 27.8 %all-gather.75.cloned.1.call-done = f32[1024,256]{1,0:T(8,128)} async-done(((f32[512,256]{1,0:T(8,128)}), f32[1024,256]{1,0:T(8,128)}) %all-gather.75.cloned.1.call-update) | async-done | bytes 1048592 | tf_op jit(solution)/shard_map/all_gather | solution.py:25
  1260.9 5.2 convolution_subtract_fusion
  1266.0 5.2 fusion.8
  1271.2 5.2 fusion.5
  1276.4 12.3 all-gather.79.cloned.1.call-done
  1290.0 4.4 fusion.2
  1295.5 12.2 all_to_all.66
  1307.7 6.9 reduce_sum.231
  1319.0 6.3 copy.47
  (219 shorter events, 132.3 us)
Async XLA Ops:
  12.6 3.2 copy-start
  17.6 10.7 all-to-all-start
  25.6 117.5 %all-gather.53.cloned.1.call-start = ((), (), s32[]{:S(2)}) async-start(), calls=%async_computation.15 | async-start | bytes 9437184 | tf_op jit(solution)/shard_map/all_gather | solution.py:46
  31.2 167.3 %all-gather.55.cloned.1.call-start = ((), (), s32[]{:S(2)}) async-start(), calls=%async_computation.16 | async-start | bytes 4718592 | tf_op jit(solution)/shard_map/all_gather | solution.py:25
  145.0 82.0 %all-gather.57.cloned.1.call-start = ((), (), s32[]{:S(2)}) async-start(), calls=%async_computation.17 | async-start | bytes 1572864 | tf_op jit(solution)/shard_map/all_gather | solution.py:25
  201.9 257.2 %all-gather.37.cloned.1.call-start = ((), (), s32[]{:S(2)}) async-start(), calls=%async_computation.7 | async-start | bytes 4718592 | tf_op jit(solution)/shard_map/all_gather | solution.py:25
  238.5 1.0 copy-start.13
  322.4 4.0 copy-start.12
  326.5 55.2 %copy-start.5 = (f32[512,512]{1,0:T(8,128)S(1)}, f32[512,512]{1,0:T(8,128)}, u32[]{:S(2)}) copy-start(f32[512,512]{1,0:T(8,128)} %fusion.28) | copy-start | bytes 3145732
  340.8 0.7 copy-start.18
  383.3 4.2 copy-start.15
  390.7 8.0 copy-start.3
  403.7 83.9 %all-gather.59.cloned.1.call-start = ((), (), s32[]{:S(2)}) async-start(), calls=%async_computation.18 | async-start | bytes 1572864 | tf_op jit(solution)/shard_map/all_gather | solution.py:25
  462.5 150.4 %all-gather.61.cloned.1.call-start = ((), (), s32[]{:S(2)}) async-start(), calls=%async_computation.19 | async-start | bytes 9437184 | tf_op jit(solution)/shard_map/all_gather | solution.py:46
  492.8 1.3 copy-start.2
  501.2 167.0 %all-gather.63.cloned.1.call-start = ((), (), s32[]{:S(2)}) async-start(), calls=%async_computation.20 | async-start | bytes 4718592 | tf_op jit(solution)/shard_map/all_gather | solution.py:25
  614.9 82.0 %all-gather.65.cloned.1.call-start = ((), (), s32[]{:S(2)}) async-start(), calls=%async_computation.21 | async-start | bytes 1572864 | tf_op jit(solution)/shard_map/all_gather | solution.py:25
  671.8 196.4 %all-gather.41.cloned.1.call-start = ((), (), s32[]{:S(2)}) async-start(), calls=%async_computation.9 | async-start | bytes 4718592 | tf_op jit(solution)/shard_map/all_gather | solution.py:25
  672.5 199.0 %all-gather.45.cloned.1.call-start = ((), (), s32[]{:S(2)}) async-start(), calls=%async_computation.11 | async-start | bytes 4718592 | tf_op jit(solution)/shard_map/all_gather | solution.py:25
  673.1 201.9 %all-gather.49.cloned.1.call-start = ((), (), s32[]{:S(2)}) async-start(), calls=%async_computation.13 | async-start | bytes 4718592 | tf_op jit(solution)/shard_map/all_gather | solution.py:25
  673.9 248.3 %all-gather.39.cloned.1.call-start = ((), (), s32[]{:S(2)}) async-start(), calls=%async_computation.8 | async-start | bytes 4718592 | tf_op jit(solution)/shard_map/all_gather | solution.py:25
  704.3 1.0 copy-start.14
  792.8 53.9 %copy-start.6 = (f32[512,512]{1,0:T(8,128)S(1)}, f32[512,512]{1,0:T(8,128)}, u32[]{:S(2)}) copy-start(f32[512,512]{1,0:T(8,128)} %fusion.28) | copy-start | bytes 3145732
  866.8 110.6 %all-gather.43.cloned.1.call-start = ((), (), s32[]{:S(2)}) async-start(), calls=%async_computation.10 | async-start | bytes 4718592 | tf_op jit(solution)/shard_map/all_gather | solution.py:25
  867.5 164.9 %all-gather.47.cloned.1.call-start = ((), (), s32[]{:S(2)}) async-start(), calls=%async_computation.12 | async-start | bytes 4718592 | tf_op jit(solution)/shard_map/all_gather | solution.py:25
  868.1 190.9 %all-gather.69.cloned.1.call-start = ((), (), s32[]{:S(2)}) async-start(), calls=%async_computation.23 | async-start | bytes 1572864 | tf_op jit(solution)/shard_map/all_gather | solution.py:25
  871.5 216.5 %all-gather.73.cloned.1.call-start = ((), (), s32[]{:S(2)}) async-start(), calls=%async_computation.25 | async-start | bytes 1572864 | tf_op jit(solution)/shard_map/all_gather | solution.py:25
  875.0 242.1 %all-gather.77.cloned.1.call-start = ((), (), s32[]{:S(2)}) async-start(), calls=%async_computation.27 | async-start | bytes 1572864 | tf_op jit(solution)/shard_map/all_gather | solution.py:25
  878.4 296.1 %all-gather.51.cloned.1.call-start = ((), (), s32[]{:S(2)}) async-start(), calls=%async_computation.14 | async-start | bytes 4718592 | tf_op jit(solution)/shard_map/all_gather | solution.py:25
  878.9 322.3 %all-gather.67.cloned.1.call-start = ((), (), s32[]{:S(2)}) async-start(), calls=%async_computation.22 | async-start | bytes 1572864 | tf_op jit(solution)/shard_map/all_gather | solution.py:25
  925.5 304.8 %all-gather.71.cloned.1.call-start = ((), (), s32[]{:S(2)}) async-start(), calls=%async_computation.24 | async-start | bytes 1572864 | tf_op jit(solution)/shard_map/all_gather | solution.py:25
  980.7 278.8 %all-gather.75.cloned.1.call-start = ((), (), s32[]{:S(2)}) async-start(), calls=%async_computation.26 | async-start | bytes 1572864 | tf_op jit(solution)/shard_map/all_gather | solution.py:25
  1035.7 252.9 %all-gather.79.cloned.1.call-start = ((), (), s32[]{:S(2)}) async-start(), calls=%async_computation.28 | async-start | bytes 1572864 | tf_op jit(solution)/shard_map/all_gather | solution.py:25
  1119.2 4.3 copy-start.16
  1123.5 3.2 copy-start.17
  1260.9 5.2 copy-start.8
  1266.0 5.2 copy-start.7
  1290.0 4.4 copy-start.9
  1290.0 4.4 copy-start.10
  1290.0 4.4 copy-start.11
  1314.6 3.4 copy-start.1
  1314.6 3.7 copy-start.4
Sparse Core Ops, SparseCore 0:
  31.3 111.8 all-gather.52
  145.2 53.2 all-gather.54
  202.1 24.9 all-gather.56
  403.8 55.2 all-gather.36
  462.6 24.9 all-gather.58
  501.4 111.5 all-gather.60
  615.0 53.2 all-gather.62
  671.9 24.9 all-gather.64
  698.7 55.7 all-gather.40
  756.1 53.6 all-gather.44
  811.6 53.5 all-gather.48
  866.9 55.2 all-gather.38
  924.0 53.3 all-gather.42
  979.0 53.3 all-gather.46
  1034.0 24.9 all-gather.68
  1060.7 27.3 all-gather.72
  1089.7 27.3 all-gather.76
  1118.7 55.7 all-gather.50
  1176.3 24.9 all-gather.66
  1202.9 27.3 all-gather.70
  1232.1 27.3 all-gather.74
  1261.3 27.3 all-gather.78
